TPU v7x, 32 devices: a whole 2x2x4 slice. The times are simulated.
32 devices in a mesh: rows: 8 (over z, x), grp: 4 (over y, core).
Axes of the slice: x: 2, y: 2, z: 4, core: 2. Of those that a mesh axis runs over, the one named last changes fastest.
Arguments:
- matrix: bfloat16 [10240, 16384], P(('rows', 'grp')), may hold values from -36 to 36
- sample_rows: int32 [32, 128, 256], P(('rows', 'grp')), may hold values from 0 to 319
- pair_list: int32 [8, 8, 4], replicated, may hold values from 0 to 255, as said below
- pair_count: int32 [8, 8], replicated, may hold values from 1 to 4, as said below
- pair_blocks: int32 [256, 2], replicated, may hold values from 0 to 127, as said below
Outputs:
- gram: float32 [256, 128, 128], P(('rows', 'grp'))
Inputs may be any that keep to these rules, and one draw needn't show every extreme that they name: `pair_list`: entry [s, r, k] lies in [r * 32, (r + 1) * 32); the 4 entries of one [s, r] are distinct. `pair_count`: every row group has some owner with all 4 slots active, and some owner has all 4 slots active from every row group. `pair_blocks`: the two blocks of a pair differ.
All inputs are finite; a program needn't handle non-finite values.
Results may differ from a plain program's by a relative error of at most 0.0016.
Values sent between devices are 32-bit elements; how exact they have to be, the bound alone decides.
A program may use at most 192 MiB of HBM per device.

v0:
```python
import functools

import jax
import jax.numpy as jnp
from jax import lax
from jax.experimental import pallas as pl
from jax.experimental.pallas import tpu as pltpu
from jax.sharding import PartitionSpec as P

epsilon = 1e-06
MESH = pl.DeviceIdType.MESH
F32 = jnp.float32
BF16 = jnp.bfloat16


def kernel(
    dims, pair_list, pair_count, pair_blocks, samples_hbm, matrix, out,
    mat, samples, sample_sem, squares, sq_in, sq_half, sq_in2, sq_rows, sq_total,
    core_out, core_in, keep, high_in, row_in0, row_in1, part_a, part_b, part_c, part_d, in_a, in_b, in_c,
    load_sem, sq_send, sq_recv, sq_row_send, sq_row_recv,
    core_send, core_recv, high_send, high_recv, row_send, row_recv,
    a_send, a_recv, b_send, b_recv, c_send, c_recv,
):
    row_count, grp_count, cap, pairs = dims
    block_count, rows_dev, width = mat.shape
    sample_count = samples.shape[1]
    half = cap // 2
    region = pairs // row_count
    tile_dev = region // grp_count
    quota = half // 2
    row_half = row_count // 2

    s = lax.axis_index("rows")
    g = lax.axis_index("grp")
    low = lax.rem(g, 2)
    high = lax.div(g, 2)
    partner = high * 2 + (1 - low)
    across = (1 - high) * 2 + low

    def at(row, grp):
        return {"rows": row, "grp": grp}

    def send(source, target, send_sem, recv_sem, row, grp):
        return pltpu.make_async_remote_copy(
            src_ref=source, dst_ref=target, send_sem=send_sem, recv_sem=recv_sem,
            device_id=at(row, grp), device_id_type=MESH,
        )

    def load(i):
        source = matrix.at[:, pl.ds(pl.multiple_of(i * width, width), width)]
        return pltpu.make_async_copy(source, mat.at[i], load_sem.at[i])

    def load_go(i, carry):
        load(i).start()
        return carry

    sample_load = pltpu.make_async_copy(samples_hbm, samples, sample_sem)
    sample_load.start()
    lax.fori_loop(0, block_count, load_go, 0)

    barrier = pltpu.get_barrier_semaphore()
    pl.semaphore_signal(barrier, inc=1, device_id=at(s, partner), device_id_type=MESH)
    pl.semaphore_signal(barrier, inc=1, device_id=at(s, across), device_id_type=MESH)

    def greet(j, carry):
        row = lax.rem(s + j, row_count)
        pl.semaphore_signal(barrier, inc=1, device_id=at(row, g), device_id_type=MESH)
        return carry

    lax.fori_loop(1, row_count, greet, 0)

    row_in = (row_in0, row_in1)
    tall = width // 2
    lines_of = (pl.ds(0, tall), pl.ds(tall, tall))
    zero_tile = jnp.zeros((tall, width), F32)

    def clear(j, carry):
        for h in range(2):
            row_in[h][j, half] = zero_tile
        return carry

    lax.fori_loop(0, row_count, clear, 0)

    def square_group(n, carry):
        lines = []
        for m in range(8):
            load(n * 8 + m).wait()
        for m in range(8):
            values = mat[n * 8 + m].astype(F32)
            lines.append(jnp.sum(values * values, axis=0, keepdims=True))
        squares[pl.ds(pl.multiple_of(n * 8, 8), 8), :] = jnp.concatenate(lines, axis=0)
        return carry

    lax.fori_loop(0, block_count // 8, square_group, 0)
    sample_load.wait()
    pl.semaphore_wait(barrier, row_count + 1)

    nb2 = block_count // 2
    nb4 = block_count // 4

    def span(start, size):
        return pl.ds(pl.multiple_of(start, 8), size)

    sq1 = send(squares.at[span((1 - low) * nb2, nb2)], sq_in, sq_send.at[0], sq_recv.at[0], s, partner)
    sq2 = send(sq_half.at[span((1 - high) * nb4, nb4)], sq_in2, sq_send.at[1], sq_recv.at[1], s, across)
    quarter = span(low * nb2 + high * nb4, nb4)
    sq4 = send(sq_total.at[quarter], sq_total.at[quarter], sq_send.at[2], sq_recv.at[2], s, across)
    my_half = span(low * nb2, nb2)
    sq5 = send(sq_total.at[my_half], sq_total.at[my_half], sq_send.at[3], sq_recv.at[3], s, partner)

    def sq_row(j):
        row = lax.rem(s + j, row_count)
        return send(sq_rows.at[s], sq_rows.at[s], sq_row_send.at[j], sq_row_recv.at[s], row, g)

    def sq_row_from(j):
        source = lax.rem(s + j, row_count)
        return send(sq_rows.at[source], sq_rows.at[source], sq_row_send.at[j], sq_row_recv.at[source], source, g)

    positions = lax.broadcasted_iota(jnp.int32, (rows_dev, sample_count), 0)
    ones = jnp.ones((sample_count, width), BF16)

    def slot_tile(owner, slot):
        pair = pair_list[s, slot, owner]
        active = (slot < pair_count[s, owner]).astype(F32)
        first = pair_blocks[0, pair]
        second = pair_blocks[1, pair]
        picked = samples[first].reshape(1, sample_count)
        hits = jnp.where(positions == picked, 1.0, 0.0).astype(BF16)
        multiplicity = jnp.dot(hits, ones, preferred_element_type=F32)
        left = mat[first].astype(F32)
        right = mat[second]
        weighted = (multiplicity * active * left).astype(BF16)
        return lax.dot_general(
            weighted, right, (((0,), (0,)), ((), ())), preferred_element_type=F32
        )

    def core_copy(j):
        return send(core_out.at[j], core_in.at[j], core_send.at[j], core_recv.at[j], s, partner)

    top = lax.div(s, row_half)

    def far(j):
        return (1 - top) * row_half + lax.rem(s + j, row_half)

    def near(j):
        return top * row_half + lax.rem(s + j, row_half)

    mine = pl.ds(high * quota, quota)
    theirs = pl.ds((1 - high) * quota, quota)
    whole = pl.ds(0, half)
    last = row_count - 1

    def is_far(k):
        return k < row_half

    def is_near(k):
        return (k >= row_half) & (k < last)

    def high_copy(k):
        return send(keep.at[k, theirs], high_in.at[k], high_send.at[k], high_recv.at[k], s, across)

    def far_copy(h, j):
        k = j
        return send(
            keep.at[k, mine, lines_of[h]], row_in[h].at[s, mine],
            row_send.at[h * row_count + k], row_recv.at[h * row_count + s], far(j), g,
        )

    def far_from(h, j):
        k = j
        source = far(j)
        return send(
            keep.at[k, mine, lines_of[h]], row_in[h].at[source, mine],
            row_send.at[h * row_count + k], row_recv.at[h * row_count + source], source, g,
        )

    def near_copy(h, j):
        k = row_half + j - 1
        return send(
            keep.at[k, whole, lines_of[h]], row_in[h].at[s, whole],
            row_send.at[h * row_count + k], row_recv.at[h * row_count + s], near(j), g,
        )

    def near_from(h, j):
        k = row_half + j - 1
        source = near(j)
        return send(
            keep.at[k, whole, lines_of[h]], row_in[h].at[source, whole],
            row_send.at[h * row_count + k], row_recv.at[h * row_count + source], source, g,
        )

    def owner_of(k):
        other = 1 - lax.div(k, row_half)
        j = k + 1 - other
        return (top * (1 - other) + (1 - top) * other) * row_half + lax.rem(s + j, row_half)

    def make(k):
        owner = owner_of(k)
        sent = [slot_tile(owner, (1 - low) * half + n) for n in range(half)]
        kept = [slot_tile(owner, low * half + n) for n in range(half)]
        for n in range(half):
            core_out[k, n] = sent[n]
        core_copy(k).start()
        for n in range(half):
            keep[k, n] = kept[n]

    def fold(k):
        core_copy(k).wait_recv()
        keep[k] = keep[k] + core_in[k]

    def cross(k):
        high_copy(k).wait_recv()
        keep[k, mine] = keep[k, mine] + high_in[k]
        far_copy(0, k).start()

    sq1.start()
    fold_lag, cross_lag = 1, 3

    def step(i, carry):
        @pl.when(i < row_count)
        def _():
            make(i)

        @pl.when(i == 1)
        def _():
            sq1.wait()
            sq_half[...] = squares[my_half, :] + sq_in[...]
            sq2.start()

        k = i - fold_lag

        @pl.when((k >= 0) & (k < row_count))
        def _():
            fold(k)

            @pl.when(is_far(k))
            def _():
                high_copy(k).start()

            @pl.when(is_near(k))
            def _():
                near_copy(0, k - row_half + 1).start()

        @pl.when(i == 4)
        def _():
            sq2.wait()
            sq_rows[s] = sq_half[span(high * nb4, nb4), :] + sq_in2[...]

            def sq_go(j, carry):
                sq_row(j).start()
                return carry

            lax.fori_loop(1, row_count, sq_go, 0)

        m = i - cross_lag

        @pl.when((m >= 0) & (m < row_count))
        def _():
            @pl.when(is_far(m))
            def _():
                cross(m)

        return carry

    lax.fori_loop(0, row_count + fold_lag, step, 0)

    def second_far(j, carry):
        far_copy(1, j).start()
        return carry

    def second_near(j, carry):
        near_copy(1, j).start()
        return carry

    lax.fori_loop(0, row_half, second_far, 0)
    lax.fori_loop(1, row_half, second_near, 0)
    for h in range(2):
        row_in[h][s, whole] = keep[last, whole, lines_of[h]]

    def sq_done(j, carry):
        sq_row_from(j).wait_recv()
        return carry

    lax.fori_loop(1, row_count, sq_done, 0)
    sq_sum = sq_rows[0]
    for j in range(1, row_count):
        sq_sum = sq_sum + sq_rows[j]
    sq_total[quarter, :] = sq_sum
    sq4.start()

    def arrive(h):
        def near_done(j, carry):
            near_from(h, j).wait_recv()
            return carry

        def far_done(j, carry):
            far_from(h, j).wait_recv()
            return carry

        lax.fori_loop(1, row_half, near_done, 0)
        lax.fori_loop(0, row_half, far_done, 0)

    def owned(h, grp, n):
        pair = s * region + grp * tile_dev + n
        total = None
        for j in range(row_count):
            source = far(j) if j < row_half else near(j - row_half)
            index = half
            for m in range(quota if j < row_half else half):
                place = m + high * quota if j < row_half else m
                same = (pair_list[source, low * half + place, s] == pair).astype(jnp.int32)
                index = jnp.minimum(index, half - (half - place) * same)
            tile = row_in[h][source, index]
            total = tile if total is None else total + tile
        return total

    def a_copy(h, n):
        k = h * tile_dev + n
        lines = lines_of[h]
        return send(part_a.at[n, lines], in_a.at[n, lines], a_send.at[k], a_recv.at[k], s, partner)

    def b_copy(h, n):
        k = h * tile_dev + n
        lines = lines_of[h]
        return send(part_b.at[n, lines], in_b.at[n, lines], b_send.at[k], b_recv.at[k], s, across)

    def c_copy(h):
        lines = lines_of[h]
        return send(part_c.at[:, lines], in_c.at[:, lines], c_send.at[h], c_recv.at[h], s, partner)

    far_low = (1 - high) * 2 + low
    far_other = (1 - high) * 2 + (1 - low)

    def combine(h):
        lines = lines_of[h]

        def pass_on(n):
            a_copy(h, n).wait_recv()
            part_b[n, lines] = part_b[n, lines] + in_a[n, lines]
            b_copy(h, n).start()

        def distant(n, carry):
            @pl.when(n < tile_dev)
            def _():
                part_a[n, lines] = owned(h, far_other, n)
                a_copy(h, n).start()
                part_b[n, lines] = owned(h, far_low, n)

            @pl.when(n >= 3)
            def _():
                pass_on(n - 3)

            return carry

        def near_other(n, carry):
            part_c[n, lines] = owned(h, partner, n)
            return carry

        def local(n, carry):
            part_d[n, lines] = owned(h, g, n)
            return carry

        lax.fori_loop(0, tile_dev + 3, distant, 0)
        lax.fori_loop(0, tile_dev, near_other, 0)
        c_copy(h).start()
        lax.fori_loop(0, tile_dev, local, 0)

    arrive(0)
    combine(0)
    sq4.wait()
    sq5.start()
    arrive(1)
    combine(1)
    sq5.wait()
    sq_total[...] = jnp.sqrt(
        sq_total[...] / (rows_dev * row_count * grp_count) + epsilon
    )
    for h in range(2):
        lines = lines_of[h]
        c_copy(h).wait()

        def finish(n, carry):
            pair = s * region + g * tile_dev + n
            first = pair_blocks[0, pair]
            second = pair_blocks[1, pair]
            left = jnp.broadcast_to(sq_total[first].reshape(1, width), (width, width)).T
            right = sq_total[second].reshape(1, width)
            b_copy(h, n).wait_recv()
            total = part_d[n, lines] + in_c[n, lines] + in_b[n, lines]
            scale = sample_count * left[h * tall : (h + 1) * tall] * right
            out[n, lines] = total / scale
            return carry

        lax.fori_loop(0, tile_dev, finish, 0)

        def drain_tiles(n, carry):
            a_copy(h, n).wait_send()
            b_copy(h, n).wait_send()
            return carry

        lax.fori_loop(0, tile_dev, drain_tiles, 0)

    def drain_rows(j, carry):
        core_copy(j).wait_send()
        sq_row(j).wait_send()
        return carry

    def drain_far(j, carry):
        high_copy(j).wait_send()
        for h in range(2):
            far_copy(h, j).wait_send()
        return carry

    def drain_near(j, carry):
        for h in range(2):
            near_copy(h, j).wait_send()
        return carry

    lax.fori_loop(1, row_count, drain_rows, 0)
    core_copy(0).wait_send()
    lax.fori_loop(0, row_half, drain_far, 0)
    lax.fori_loop(1, row_half, drain_near, 0)


def shards(matrix, sample_rows, pair_list, pair_count, pair_blocks):
    rows_dev, column_count = matrix.shape
    block_count, sample_count = sample_rows.shape[1:]
    width = column_count // block_count
    row_count = lax.axis_size("rows")
    grp_count = lax.axis_size("grp")
    cap = pair_list.shape[2]
    pairs = pair_blocks.shape[0]
    tile_dev = pairs // (row_count * grp_count)
    half = cap // 2
    dma = pltpu.SemaphoreType.DMA

    def vmem(*shape):
        return pltpu.VMEM(shape, F32)

    some = vmem(tile_dev, width, width)
    nb2, nb4 = block_count // 2, block_count // 4
    return pl.pallas_call(
        functools.partial(kernel, (row_count, grp_count, cap, pairs)),
        out_shape=jax.ShapeDtypeStruct((tile_dev, width, width), F32),
        in_specs=[
            pl.BlockSpec(memory_space=pltpu.SMEM),
            pl.BlockSpec(memory_space=pltpu.SMEM),
            pl.BlockSpec(memory_space=pltpu.SMEM),
            pl.BlockSpec(memory_space=pl.ANY),
            pl.BlockSpec(memory_space=pl.ANY),
        ],
        out_specs=pl.BlockSpec(memory_space=pltpu.VMEM),
        scratch_shapes=[
            pltpu.VMEM((block_count, rows_dev, width), BF16),
            pltpu.VMEM((block_count, sample_count), jnp.int32),
            dma,
            vmem(block_count, width),
            vmem(nb2, width),
            vmem(nb2, width),
            vmem(nb4, width),
            vmem(row_count, nb4, width),
            vmem(block_count, width),
            vmem(row_count, half, width, width),
            vmem(row_count, half, width, width),
            vmem(row_count, half, width, width),
            vmem(row_count, half // 2, width, width),
            vmem(row_count, half + 1, width // 2, width),
            vmem(row_count, half + 1, width // 2, width),
            some, some, some, some, some, some, some,
            dma((block_count,)), dma((4,)), dma((4,)), dma((row_count,)), dma((row_count,)),
            dma((row_count,)), dma((row_count,)), dma((row_count,)), dma((row_count,)),
            dma((2 * row_count,)), dma((2 * row_count,)),
            dma((2 * tile_dev,)), dma((2 * tile_dev,)), dma((2 * tile_dev,)),
            dma((2 * tile_dev,)), dma((2,)), dma((2,)),
        ],
        compiler_params=pltpu.CompilerParams(
            collective_id=0, has_side_effects=True, vmem_limit_bytes=67043328
        ),
        name="gram_tiles",
    )(pair_list.transpose(0, 2, 1), pair_count, pair_blocks.T, sample_rows[0], matrix)


def solution(mesh):
    in_specs = (P(("rows", "grp"), None), P(("rows", "grp"), None, None), P(), P(), P())
    out_specs = P(("rows", "grp"), None, None)
    return jax.shard_map(shards, mesh=mesh, in_specs=in_specs, out_specs=out_specs, check_vma=False)
```

profile of v0, /device:TPU:0, one launch (start us, length us, event | category | flops | bytes accessed | tf_op | source)
XLA Modules:
  0.0 45.2 jit_solution(12142331262696959798)
XLA Ops:
  0.0 43.3 %gram_tiles.1 = f32[8,128,128]{2,1,0:T(8,128)} custom-call(s32[8,4,8]{2,1,0:T(4,128)} %bitcast.4, s32[8,8]{1,0:T(8,128)} %pair_count.1, s32[2,256]{1,0:T(2,128)} %bitcast.5, s32[128,256]{1,0:T(8,128)} %bitcast.3, bf16[320,16384]{1,0:T(8,128)(2,1)} %matrix.1), custom_call_target="tpu_custom_call" | custom-call | tf_op jit(solution)/shard_map/gram_tiles/pallas_call | solution.py:442
  43.3 1.9 %copy.7 = f32[8,128,128]{2,1,0:T(8,128)} copy(f32[8,128,128]{2,1,0:T(8,128)} %gram_tiles.1) | data formatting | bytes 1048576
where the time goes:
time: 45.6 us; the launch traced here: 45.2 us
  Pallas kernels  43.3 us (95%)
  local copies, waits for them, and re-layouts  1.87 us (4%)
    pallas_call x1, Pallas kernels, shards(): pl.pallas_call(functools.partial(kernel, (row_count, grp_count, cap, pair...  43.3 us
    unnamed x1, local copies, waits for them, and re-layouts  1.87 us

commit v1 on v0

v1 whole, which is shorter than its diff:
```python
import functools

import jax
import jax.numpy as jnp
from jax import lax
from jax.experimental import pallas as pl
from jax.experimental.pallas import tpu as pltpu
from jax.sharding import PartitionSpec as P

epsilon = 1e-06
MESH = pl.DeviceIdType.MESH
F32 = jnp.float32
BF16 = jnp.bfloat16
CHUNKS = 4
LOADS = 8
FOLD_LAG = 3
CROSS_LAG = 6
EARLY = 6
scope = jax.named_scope


def kernel(
    dims, list_hbm, count_hbm, blocks_hbm, samples_hbm, matrix, out, *scratch,
):
    row_count, grp_count, cap, pairs, pre = dims
    it = iter(scratch)
    mat, samples, counts, places, tiles, core_in, high_in = [next(it) for _ in range(7)]
    row_in = [next(it) for _ in range(CHUNKS)]
    part_b, in_b, held, part_c, in_c, scale = [next(it) for _ in range(6)]
    squares, sq_in, sq_half, sq_in2, sq_rows, sq_sum, sq_far, sq_total = [next(it) for _ in range(8)]
    pair_list, pair_count, pair_blocks = [next(it) for _ in range(3)]
    (table_sem, sample_sem, load_sem, sq_send, sq_recv, near_send, near_recv, core_send, core_recv,
     high_send, high_recv, row_send, row_recv, b_send, b_recv, c_send, c_recv) = it

    block_count, rows_dev, width = mat.shape
    sample_count = samples.shape[1]
    half = cap // 2
    region = pairs // row_count
    tile_dev = region // grp_count
    row_half = row_count // 2
    tall = width // 2
    thin = tall // CHUNKS

    s = lax.axis_index("rows")
    g = lax.axis_index("grp")
    low = lax.rem(g, 2)
    high = lax.div(g, 2)
    partner = high * 2 + (1 - low)
    across = (1 - high) * 2 + low

    def send(source, target, send_sem, recv_sem, row, grp):
        return pltpu.make_async_remote_copy(
            src_ref=source, dst_ref=target, send_sem=send_sem, recv_sem=recv_sem,
            device_id={"rows": row, "grp": grp}, device_id_type=MESH,
        )

    def await_bytes(ref, sem):
        pltpu.make_async_copy(ref, ref, sem).wait()

    def lines_from(start, size):
        return pl.ds(pl.multiple_of(start, 8), size)

    with scope("greet"):
        barrier = pltpu.get_barrier_semaphore()
        pl.semaphore_signal(barrier, inc=1, device_id={"rows": s, "grp": partner}, device_id_type=MESH)
        pl.semaphore_signal(barrier, inc=1, device_id={"rows": s, "grp": across}, device_id_type=MESH)

        def greet(j, carry):
            row = lax.rem(s + j, row_count)
            pl.semaphore_signal(barrier, inc=1, device_id={"rows": row, "grp": g}, device_id_type=MESH)
            return carry

        lax.fori_loop(1, row_count, greet, 0)

    batch = block_count // LOADS

    def load_go(i, carry):
        source = matrix.at[:, pl.ds(pl.multiple_of(i * width, width), width)]
        pltpu.make_async_copy(source, mat.at[i], load_sem.at[lax.div(i, batch)]).start()
        return carry

    with scope("issue"):
        tables = [
            pltpu.make_async_copy(source, target, table_sem.at[n])
            for n, (source, target) in enumerate(
                ((list_hbm, pair_list), (count_hbm, pair_count), (blocks_hbm, pair_blocks))
            )
        ]
        sample_load = pltpu.make_async_copy(samples_hbm, samples, sample_sem)
        sample_load.start()
        for table in tables:
            table.start()
        lax.fori_loop(0, block_count, load_go, 0)

    top = lax.div(s, row_half)

    def owner_of(k):
        other = 1 - lax.div(k, row_half)
        j = k + 1 - other
        return (top * (1 - other) + (1 - top) * other) * row_half + lax.rem(s + j, row_half)

    zero_tile = jnp.zeros((thin, width), F32)

    def clear(j, carry):
        for q in range(CHUNKS):
            row_in[q][j, cap] = zero_tile
        return carry

    lax.fori_loop(0, row_count, clear, 0)

    def source_of(k):
        return ((1 - top) if k < row_half else top) * row_half + lax.rem(s + k, row_half)

    def place(j, carry):
        pair = s * region + j
        for k in range(row_count):
            source = source_of(k)
            slot = cap
            for n in range(half if k < row_half else cap):
                at = high * half + n if k < row_half else n
                slot = jnp.where(pair_list[source, at, s] == pair, at, slot)
            places[j, k] = slot
        return carry

    with scope("w_samples"):
        sample_load.wait()
        for table in tables:
            table.wait()

    positions = lax.broadcasted_iota(jnp.int32, (rows_dev, sample_count), 0)
    ones = jnp.ones((sample_count, width), BF16)

    def count(owner, slot):
        first = pair_blocks[0, pair_list[s, slot, owner]]
        active = (slot < pair_count[s, owner]).astype(F32)
        picked = samples[first].reshape(1, sample_count)
        hits = jnp.where(positions == picked, 1.0, 0.0).astype(BF16)
        multiplicity = jnp.dot(hits, ones, preferred_element_type=F32)
        return (multiplicity * active).astype(BF16)

    def count_owner(k, carry):
        owner = owner_of(k)
        for n in range(cap):
            counts[lax.rem(k, pre), n] = count(owner, n)
        return carry

    with scope("counts"):
        lax.fori_loop(0, pre, count_owner, 0)

    def square_group(n, carry):
        lines = []
        for m in range(8):
            values = mat[n * 8 + m].astype(F32)
            lines.append(jnp.sum(values * values, axis=0, keepdims=True))
        squares[lines_from(n * 8, 8), :] = jnp.concatenate(lines, axis=0)
        return carry

    with scope("load_sq"):
        for i in range(LOADS):
            with scope("w_load"):
                await_bytes(mat.at[pl.ds(i * batch, batch)], load_sem.at[i])
            if i < EARLY:
                lax.fori_loop(i * batch // 8, (i + 1) * batch // 8, square_group, 0)

    nb2 = block_count // 2
    nb4 = block_count // 4
    my_half = lines_from(low * nb2, nb2)
    quarter = lines_from(low * nb2 + high * nb4, nb4)

    sq1 = send(squares.at[lines_from((1 - low) * nb2, nb2)], sq_in, sq_send.at[0], sq_recv.at[0], s, partner)
    sq2 = send(sq_half.at[lines_from((1 - high) * nb4, nb4)], sq_in2, sq_send.at[1], sq_recv.at[1], s, across)
    sq4 = send(sq_total.at[quarter], sq_total.at[quarter], sq_send.at[2], sq_recv.at[2], s, across)
    sq5 = send(sq_total.at[my_half], sq_total.at[my_half], sq_send.at[3], sq_recv.at[3], s, partner)

    def near_row(j):
        return top * row_half + lax.rem(s + j, row_half)

    def sq_near(j):
        return send(sq_rows.at[s], sq_rows.at[s], near_send, near_recv, near_row(j), g)

    def sq_near_go(j, carry):
        sq_near(j).start()
        return carry

    sq3 = send(sq_sum, sq_far, sq_send.at[4], sq_recv.at[4], (1 - top) * row_half + lax.rem(s, row_half), g)

    def sq_first():
        sq1.wait()
        sq_half[...] = squares[my_half, :] + sq_in[...]
        sq2.start()

    def sq_second():
        sq2.wait()
        sq_rows[s] = sq_half[lines_from(high * nb4, nb4), :] + sq_in2[...]
        lax.fori_loop(1, row_half, sq_near_go, 0)

    def sq_third():
        await_bytes(sq_rows.at[pl.ds(0, row_half - 1)], near_recv)
        total = sq_rows[near_row(0)]
        for j in range(1, row_half):
            total = total + sq_rows[near_row(j)]
        sq_sum[...] = total
        sq3.start()

    def sq_next():
        sq3.wait()
        sq_total[quarter, :] = sq_sum[...] + sq_far[...]
        sq4.start()

    def sq_fourth():
        sq4.wait()
        sq5.start()

    my_lines = lines_from(low * tall, tall)
    their_lines = lines_from((1 - low) * tall, tall)
    mine = pl.ds(high * half, half)
    theirs = pl.ds((1 - high) * half, half)
    every = pl.ds(0, cap)

    def lines(q):
        return lines_from(low * tall + q * thin, thin)

    def core_copy(k):
        return send(tiles.at[k, every, their_lines], core_in.at[k], core_send, core_recv.at[k], s, partner)

    def high_copy(k, q):
        target = high_in.at[k, pl.ds(0, half), pl.ds(q * thin, thin)]
        return send(tiles.at[k, theirs, lines(q)], target, high_send, high_recv.at[k * CHUNKS + q], s, across)

    def far_copy(k, q):
        return send(tiles.at[k, mine, lines(q)], row_in[q].at[s, mine], row_send, row_recv.at[q], owner_of(k), g)

    def near_copy(k, q):
        return send(tiles.at[k, every, lines(q)], row_in[q].at[s, every], row_send, row_recv.at[q], owner_of(k), g)

    def make(k):
        owner = owner_of(k)
        for n in range(cap):
            pair = pair_list[s, n, owner]
            left = mat[pair_blocks[0, pair]]
            right = mat[pair_blocks[1, pair]]
            weighted = counts[lax.rem(k, pre), n] * left
            tiles[k, n] = lax.dot_general(
                weighted, right, (((0,), (0,)), ((), ())), preferred_element_type=F32
            )

    def fold(k):
        core_copy(k).wait_recv()
        tiles[k, :, my_lines] = tiles[k, :, my_lines] + core_in[k]

    def cross(k, q):
        high_copy(k, q).wait_recv()
        tiles[k, mine, lines(q)] = tiles[k, mine, lines(q)] + high_in[k, :, pl.ds(q * thin, thin)]
        far_copy(k, q).start()

    last = row_count - 1
    with scope("make"):
        make(0)
    with scope("barrier"):
        pl.semaphore_wait(barrier, row_count + 1)
    core_copy(0).start()

    def step(i, carry):
        @pl.when(i < pre)
        def _():
            with scope("make"):
                make(i)
            core_copy(i).start()

        @pl.when(i == row_half)
        def _():
            with scope("squares"):
                lax.fori_loop(EARLY * batch // 8, block_count // 8, square_group, 0)
            sq1.start()

        if pre < row_count:
            @pl.when((i >= pre) & (i < row_count))
            def _():
                with scope("make_b"):
                    count_owner(i, 0)
                    make(i)
                core_copy(i).start()

        @pl.when(i == row_half + 2)
        def _():
            with scope("sq_first"):
                sq_first()

        k = i - FOLD_LAG

        @pl.when((k >= 0) & (k < row_count))
        def _():
            with scope("fold"):
                fold(k)

            @pl.when(k < row_half)
            def _():
                high_copy(k, 0).start()

            @pl.when(k == row_half - 1)
            def _():
                for q in range(1, CHUNKS):
                    def rest(j, carry):
                        high_copy(j, q).start()
                        return carry

                    lax.fori_loop(0, row_half, rest, 0)

            @pl.when((k >= row_half) & (k < last))
            def _():
                near_copy(k, 0).start()

        m = i - CROSS_LAG

        @pl.when((m >= 0) & (m < row_half))
        def _():
            with scope("cross"):
                cross(m, 0)

        return carry

    lax.fori_loop(1, max(row_count + FOLD_LAG, row_half + CROSS_LAG), step, 0)
    for q in range(1, CHUNKS):
        def near_go(k, carry):
            near_copy(k, q).start()
            return carry

        def cross_go(k, carry):
            cross(k, q)
            return carry

        lax.fori_loop(row_half, last, near_go, 0)
        with scope("crosses"):
            lax.fori_loop(0, row_half, cross_go, 0)
        if q == 1:
            with scope("sq_second"):
                sq_second()
    with scope("places"):
        lax.fori_loop(0, region, place, 0)
    for q in range(CHUNKS):
        row_in[q][s, every] = tiles[last, :, lines(q)]

    def owned(q, grp, n):
        j = grp * tile_dev + n
        total = row_in[q][source_of(0), places[j, 0]]
        for k in range(1, row_count):
            total = total + row_in[q][source_of(k), places[j, k]]
        return total

    distant = ((1 - high) * 2 + (1 - low), (1 - high) * 2 + low)
    local = (partner, g)

    def b_copy(q, t):
        k = q * 2 + t
        return send(part_b.at[q, t], in_b.at[q, t], b_send, b_recv.at[k], s, across)

    def c_copy(q):
        return send(part_c.at[q], in_c.at[q], c_send, c_recv.at[q], s, partner)

    arriving = 3 * row_count // 4 - 1

    def post(q):
        with scope("w_rows"):
            await_bytes(row_in[q].at[pl.ds(0, arriving), every], row_recv.at[q])
        with scope("post"):
            for t in range(2):
                def away(n, carry):
                    part_b[q, t, n] = owned(q, distant[t], n)
                    return carry

                lax.fori_loop(0, tile_dev, away, 0)
                b_copy(q, t).start()
            for t in range(2):
                def hold(n, carry):
                    held[q, t, n] = owned(q, local[t], n)
                    return carry

                lax.fori_loop(0, tile_dev, hold, 0)

    def finish(q, scaled):
        with scope("w_b0"):
            b_copy(q, 0).wait_recv()
        part_c[q] = held[q, 0] + in_b[q, 0]
        c_copy(q).start()
        with scope("w_b1"):
            b_copy(q, 1).wait_recv()
        here = lines(q)
        there = lines_from((1 - low) * tall + q * thin, thin)
        own = held[q, 1] + in_b[q, 1]
        out[:, here] = own * scale[:, here] if scaled else own
        with scope("w_c"):
            c_copy(q).wait_recv()
        out[:, there] = in_c[q] * scale[:, there] if scaled else in_c[q]

    def rescale():
        sq5.wait()
        sq_total[...] = jnp.sqrt(sq_total[...] / (rows_dev * row_count * grp_count) + epsilon)

        def factor(n, carry):
            pair = (s * region + g * tile_dev) + n
            left = sq_total[pair_blocks[0, pair]].reshape(1, width)
            right = sq_total[pair_blocks[1, pair]].reshape(1, width)
            left = jnp.broadcast_to(left, (width, width)).T
            scale[n] = 1.0 / (sample_count * left * right)
            return carry

        lax.fori_loop(0, tile_dev, factor, 0)
        for q in range(CHUNKS - 1):
            for side in range(2):
                piece = pl.ds(side * tall + q * thin, thin)
                out[:, piece] = out[:, piece] * scale[:, piece]

    post(0)
    with scope("sq_third"):
        sq_third()
    post(1)
    with scope("sq_next"):
        sq_next()
    finish(0, False)
    post(2)
    with scope("sq_fourth"):
        sq_fourth()
    finish(1, False)
    post(3)
    finish(2, False)
    with scope("rescale"):
        rescale()
    finish(3, True)

    with scope("drain"):
        await_bytes(core_in, core_send)
        await_bytes(high_in, high_send)
        await_bytes(tiles.at[pl.ds(0, arriving), every, pl.ds(0, tall)], row_send)
        await_bytes(part_b, b_send)
        await_bytes(part_c, c_send)
        await_bytes(sq_rows.at[pl.ds(0, row_half - 1)], near_send)


def shards(matrix, sample_rows, pair_list, pair_count, pair_blocks):
    rows_dev, column_count = matrix.shape
    block_count, sample_count = sample_rows.shape[1:]
    width = column_count // block_count
    row_count = lax.axis_size("rows")
    grp_count = lax.axis_size("grp")
    cap = pair_list.shape[2]
    pairs = pair_blocks.shape[0]
    region = pairs // row_count
    tile_dev = region // grp_count
    half = cap // 2
    row_half = row_count // 2
    tall = width // 2
    thin = tall // CHUNKS
    pre = min(row_half, 4)
    nb2, nb4 = block_count // 2, block_count // 4
    dma = pltpu.SemaphoreType.DMA

    def vmem(*shape):
        return pltpu.VMEM(shape, F32)

    return pl.pallas_call(
        functools.partial(kernel, (row_count, grp_count, cap, pairs, pre)),
        out_shape=pltpu.VMEM((tile_dev, width, width), F32),
        in_specs=[
            pl.BlockSpec(memory_space=pl.ANY) for _ in range(5)
        ],
        out_specs=pl.BlockSpec(memory_space=pltpu.VMEM),
        scratch_shapes=[
            pltpu.VMEM((block_count, rows_dev, width), BF16),
            pltpu.VMEM((block_count, sample_count), jnp.int32),
            pltpu.VMEM((pre, cap, rows_dev, width), BF16),
            pltpu.SMEM((region, row_count), jnp.int32),
            vmem(row_count, cap, width, width),
            vmem(row_count, cap, tall, width),
            vmem(row_half, half, tall, width),
            *[vmem(row_count, cap + 1, thin, width) for _ in range(CHUNKS)],
            vmem(CHUNKS, 2, tile_dev, thin, width),
            vmem(CHUNKS, 2, tile_dev, thin, width),
            vmem(CHUNKS, 2, tile_dev, thin, width),
            vmem(CHUNKS, tile_dev, thin, width),
            vmem(CHUNKS, tile_dev, thin, width),
            vmem(tile_dev, width, width),
            vmem(block_count, width), vmem(nb2, width), vmem(nb2, width), vmem(nb4, width),
            vmem(row_count, nb4, width),
            vmem(nb4, width), vmem(nb4, width), vmem(block_count, width),
            pltpu.SMEM((row_count, cap, row_count), jnp.int32),
            pltpu.SMEM((row_count, row_count), jnp.int32),
            pltpu.SMEM((2, pairs), jnp.int32),
            dma((3,)), dma, dma((LOADS,)), dma((5,)), dma((5,)), dma, dma,
            dma, dma((row_count,)), dma, dma((row_half * CHUNKS,)),
            dma, dma((CHUNKS,)), dma, dma((2 * CHUNKS,)), dma, dma((CHUNKS,)),
        ],
        compiler_params=pltpu.CompilerParams(
            collective_id=0, has_side_effects=True, vmem_limit_bytes=60000000
        ),
        name="gram_tiles",
    )(pair_list.transpose(0, 2, 1), pair_count, pair_blocks.T, sample_rows[0], matrix)


def solution(mesh):
    in_specs = (P(("rows", "grp"), None), P(("rows", "grp"), None, None), P(), P(), P())
    out_specs = P(("rows", "grp"), None, None)
    return jax.shard_map(shards, mesh=mesh, in_specs=in_specs, out_specs=out_specs, check_vma=False)
```

time: 45.6 us -> 35.9 us (0.79)
  Pallas kernels: 43.3 us -> 34.9 us
  local copies, waits for them, and re-layouts: 1.87 us -> 0.8 us
    pallas_call x1, Pallas kernels: 43.3 us -> 34.9 us  [shards(): pl.pallas_call(functools.partial(kernel, (row_count, grp_count, cap, pair...]
    unnamed x1, local copies, waits for them, and re-layouts: 1.87 us -> 0.8 us
where the time goes in v1:
time: 35.9 us; the launch traced here: 35.7 us
  Pallas kernels  34.9 us (97%)
  local copies, waits for them, and re-layouts  0.8 us (2%)
    pallas_call x1, Pallas kernels, shards(): pl.pallas_call(functools.partial(kernel, (row_count, grp_count, cap, pair...  34.9 us
    unnamed x1, local copies, waits for them, and re-layouts  0.8 us

profile of v1, /device:TPU:0, one launch (start us, length us, event | category | flops | bytes accessed | tf_op | source)
XLA Modules:
  0.0 35.7 jit_solution(8649165873527157477)
XLA Ops:
  0.0 34.9 %gram_tiles.1 = f32[8,128,128]{2,1,0:T(8,128)S(1)} custom-call(s32[8,4,8]{2,1,0:T(4,128)} %bitcast.4, s32[8,8]{1,0:T(8,128)} %count_hbm.1, s32[2,256]{1,0:T(2,128)} %bitcast.5, s32[128,256]{1,0:T(8,128)} %bitcast.3, bf16[320,16384]{1,0:T(8,128)(2,1)} %matrix.1), custom_call_target="tpu_custom_call" | custom-call | tf_op jit(solution)/shard_map/gram_tiles/pallas_call | solution.py:460
  34.9 0.8 %copy.7 = f32[8,128,128]{2,1,0:T(8,128)} copy(f32[8,128,128]{2,1,0:T(8,128)S(1)} %gram_tiles.1) | data formatting | bytes 1048576

commit v2 on v1

v2 whole, which is shorter than its diff:
```python
import functools

import jax
import jax.numpy as jnp
from jax import lax
from jax.experimental import pallas as pl
from jax.experimental.pallas import tpu as pltpu
from jax.sharding import PartitionSpec as P

epsilon = 1e-06
MESH = pl.DeviceIdType.MESH
F32 = jnp.float32
BF16 = jnp.bfloat16
SHARES = (2, 2, 2, 2)
CHUNKS = len(SHARES)
LOADS = 8
EARLY = 8
FIRST_SQUARES = 2
scope = jax.named_scope


def kernel(
    dims, list_hbm, count_hbm, blocks_hbm, samples_hbm, matrix, out, *scratch,
):
    row_count, grp_count, cap, pairs, block_count, width = dims
    it = iter(scratch)
    mat, samples, counts, places, tiles, core_in, high_in, first_in = [next(it) for _ in range(8)]
    row_in, part_b, in_b, held, part_c, in_c = [[next(it) for _ in range(CHUNKS)] for _ in range(6)]
    place_rows, scale, squares, sq_parts, sq_rows, sq_total = [next(it) for _ in range(6)]
    pair_list, pair_count, pair_blocks = [next(it) for _ in range(3)]
    (table_sem, sample_sem, place_sem, load_sem, sq_send, sq_recv, near_send, near_recv, core_send, core_recv,
     first_send, high_send, high_recv, row_send, row_recv, b_send, b_recv, c_send, c_recv) = it

    batch = block_count // LOADS
    rows_dev = mat.shape[1]
    sample_count = samples.shape[1]
    half = cap // 2
    region = pairs // row_count
    tile_dev = region // grp_count
    row_half = row_count // 2
    tall = width // 2
    sizes = [share * tall // sum(SHARES) for share in SHARES]
    starts = [sum(sizes[:q]) for q in range(CHUNKS)]
    last = row_count - 1

    s = lax.axis_index("rows")
    g = lax.axis_index("grp")
    low = lax.rem(g, 2)
    high = lax.div(g, 2)
    partner = high * 2 + (1 - low)
    across = (1 - high) * 2 + low
    corner = (1 - high) * 2 + (1 - low)
    top = lax.div(s, row_half)

    def send(source, target, send_sem, recv_sem, row, grp):
        return pltpu.make_async_remote_copy(
            src_ref=source, dst_ref=target, send_sem=send_sem, recv_sem=recv_sem,
            device_id={"rows": row, "grp": grp}, device_id_type=MESH,
        )

    def await_bytes(ref, sem):
        pltpu.make_async_copy(ref, ref, sem).wait()

    def lines_from(start, size):
        return pl.ds(pl.multiple_of(start, 8), size)

    with scope("greet"):
        barrier = pltpu.get_barrier_semaphore()

        def greet(row, grp):
            pl.semaphore_signal(barrier, inc=1, device_id={"rows": row, "grp": grp}, device_id_type=MESH)

        def greet_row(j, carry):
            greet(lax.rem(s + j, row_count), g)
            return carry

        greet(s, partner)
        greet(s, across)
        greet(s, corner)
        for j in range(1, grp_count):
            greet(s + 1 - 2 * lax.rem(s, 2), lax.rem(g + j, grp_count))
        lax.fori_loop(1, row_count, greet_row, 0)

    with scope("issue"):
        tables = [
            pltpu.make_async_copy(source, target, table_sem.at[n])
            for n, (source, target) in enumerate(
                ((list_hbm, pair_list), (count_hbm, pair_count), (blocks_hbm, pair_blocks))
            )
        ]
        sample_load = pltpu.make_async_copy(samples_hbm, samples, sample_sem)
        sample_load.start()
        for table in tables:
            table.start()
        wide = batch * width
        for i in range(LOADS):
            pltpu.make_async_copy(matrix.at[:, pl.ds(i * wide, wide)], mat.at[i], load_sem.at[i]).start(priority=1)

    def owner_of(k):
        other = 1 - lax.div(k, row_half)
        j = k + 1 - other
        return (top * (1 - other) + (1 - top) * other) * row_half + lax.rem(s + j, row_half)

    place_copy = pltpu.make_async_copy(place_rows, places, place_sem)

    def fill_places():
        pair = s * region + lax.broadcasted_iota(jnp.int32, (1, place_rows.shape[1]), 1)
        for k in range(row_count):
            source = source_of(k)
            slot = jnp.full(pair.shape, cap, jnp.int32)
            for n in range(half if k < row_half else cap):
                at = high * half + n if k < row_half else n
                slot = jnp.where(pair == pair_list[source, at, s], at, slot)
            place_rows[k : k + 1, :] = slot
        place_copy.start()

    def source_of(k):
        return ((1 - top) if k < row_half else top) * row_half + lax.rem(s + k, row_half)

    def clear(j, carry):
        for q in range(CHUNKS):
            row_in[q][j, cap] = jnp.zeros((sizes[q], width), F32)
        return carry

    lax.fori_loop(0, row_count, clear, 0)

    with scope("w_samples"):
        sample_load.wait()
        for table in tables:
            table.wait()

    early = counts.shape[0]
    part = 128
    positions = lax.broadcasted_iota(jnp.int32, (rows_dev, part), 0)
    ones = jnp.ones((part, width), BF16)

    def count_owner(i, carry):
        owner = owner_of(i)
        for n in range(cap):
            first = pair_blocks[0, pair_list[s, n, owner]]
            active = (n < pair_count[s, owner]).astype(jnp.int32)
            picked = ((samples[first] + 1) * active - 1).reshape(1, sample_count)
            hits = None
            for c in range(sample_count // part):
                hit = jnp.where(positions == picked[:, c * part : (c + 1) * part], 1.0, 0.0)
                hits = hit if hits is None else hits + hit
            multiplicity = jnp.dot(hits.astype(BF16), ones, preferred_element_type=F32)
            counts[lax.rem(i, early), n] = multiplicity.astype(BF16)
        return carry

    with scope("places"):
        fill_places()
    with scope("counts"):
        lax.fori_loop(0, early, count_owner, 0)

    def square_batch(i, carry):
        for u in range(batch // 8):
            lines = []
            for m in range(8):
                values = mat[i, :, (u * 8 + m) * width : (u * 8 + m + 1) * width].astype(F32)
                lines.append(jnp.sum(values * values, axis=0, keepdims=True))
            squares[lines_from(i * batch + u * 8, 8), :] = jnp.concatenate(lines, axis=0)
        return carry

    def load_batch(i, carry):
        with scope("w_load"):
            await_bytes(mat.at[i], load_sem.at[i])
        return square_batch(i, carry)

    def load_wait(i, carry):
        await_bytes(mat.at[i], load_sem.at[i])
        return carry

    with scope("load_sq"):
        lax.fori_loop(0, FIRST_SQUARES, load_batch, 0)
    with scope("load_rest"):
        lax.fori_loop(FIRST_SQUARES, LOADS, load_wait, 0)

    nb8 = block_count // 8
    side = lax.rem(s, 2)
    seat = side * grp_count + g
    peers = [lax.rem(seat + j, 8) for j in range(1, 8)]

    def eighth(peer):
        grp = lax.rem(peer, grp_count)
        at = lax.rem(grp, 2) * 4 + lax.div(grp, 2) * 2 + lax.div(peer, grp_count)
        return lines_from(at * nb8, nb8)

    def peer_row(peer):
        return s - side + lax.div(peer, grp_count)

    def sq_first():
        for peer in peers:
            send(
                squares.at[eighth(peer)], sq_parts.at[seat], sq_send.at[0], sq_recv.at[0],
                peer_row(peer), lax.rem(peer, grp_count),
            ).start()

    def even_row(j):
        return lax.rem(s + 2 * j, row_count)

    def sq_second():
        await_bytes(sq_parts.at[pl.ds(0, 7)], sq_recv.at[0])
        total = squares[eighth(seat), :]
        for peer in peers:
            total = total + sq_parts[peer]
        sq_rows[s] = total

        def sq_row(j, carry):
            send(sq_rows.at[s], sq_rows.at[s], near_send, near_recv, even_row(j), g).start()
            return carry

        lax.fori_loop(1, row_half, sq_row, 0)

    def sq_third():
        await_bytes(sq_rows.at[pl.ds(0, row_half - 1)], near_recv)
        total = sq_rows[s]
        for j in range(1, row_half):
            total = total + sq_rows[even_row(j)]
        here = eighth(seat)
        sq_total[here, :] = total
        for peer in peers:
            send(
                sq_total.at[here], sq_total.at[here], sq_send.at[1], sq_recv.at[1],
                peer_row(peer), lax.rem(peer, grp_count),
            ).start()

    my_lines = lines_from(low * tall, tall)
    their_lines = lines_from((1 - low) * tall, tall)
    mine = pl.ds(high * half, half)
    theirs = pl.ds((1 - high) * half, half)
    every = pl.ds(0, cap)

    def lines(q):
        return lines_from(low * tall + starts[q], sizes[q])

    def within(q):
        return pl.ds(starts[q] - sizes[0], sizes[q])

    def core_copy(k):
        return send(tiles.at[k, every, their_lines], core_in.at[k], core_send, core_recv.at[k], s, partner)

    def high_copy(k, q):
        target = high_in.at[k, pl.ds(0, half), within(q)]
        arrived = high_recv.at[row_half + q - 1]
        return send(tiles.at[k, theirs, lines(q)], target, high_send, arrived, s, across)

    def first_copy(k, t):
        there = lines(0) if t == 0 else lines_from((1 - low) * tall, sizes[0])
        target = first_in.at[k, t]
        return send(tiles.at[k, theirs, there], target, first_send, high_recv.at[k], s, across if t == 0 else corner)

    def far_copy(k, q):
        return send(tiles.at[k, mine, lines(q)], row_in[q].at[s, mine], row_send, row_recv.at[q], owner_of(k), g)

    def near_copy(k, q):
        return send(tiles.at[k, every, lines(q)], row_in[q].at[s, every], row_send, row_recv.at[q], owner_of(k), g)

    def block(b):
        return mat[lax.div(b, batch), :, pl.ds(lax.rem(b, batch) * width, width)]

    def make(k):
        owner = owner_of(k)
        for n in range(cap):
            pair = pair_list[s, n, owner]
            weighted = counts[lax.rem(k, early), n] * block(pair_blocks[0, pair])
            tiles[k, n] = lax.dot_general(
                weighted, block(pair_blocks[1, pair]), (((0,), (0,)), ((), ())),
                preferred_element_type=F32,
            )

    later = lines_from(low * tall + sizes[0], tall - sizes[0])

    def fold_far(k):
        core_copy(k).wait_recv()
        tiles[k, :, later] = tiles[k, :, later] + core_in[k, :, sizes[0] :]
        high_copy(k, 1).start()

    def fold_near(k):
        core_copy(k).wait_recv()
        tiles[k, :, my_lines] = tiles[k, :, my_lines] + core_in[k]

    def cross_first(k):
        await_bytes(first_in.at[k], high_recv.at[k])
        own = tiles[k, mine, lines(0)] + core_in[k, mine, 0 : sizes[0]]
        tiles[k, mine, lines(0)] = own + (first_in[k, 0] + first_in[k, 1])
        far_copy(k, 0).start()

    def cross(k, q):
        tiles[k, mine, lines(q)] = tiles[k, mine, lines(q)] + high_in[k, :, within(q)]
        far_copy(k, q).start()

    def produce(k):
        if early < row_count:
            @pl.when(k >= early)
            def _():
                with scope("count"):
                    count_owner(k, 0)

        with scope("make"):
            make(k)

    def deliver(k):
        core_copy(k).start()
        for t in range(2):
            first_copy(k, t).start()

    def high_go(q):
        def go(k, carry):
            high_copy(k, q).start()
            return carry

        lax.fori_loop(0, row_half, go, 0)

    produce(0)
    with scope("barrier"):
        pl.semaphore_wait(barrier, row_count + 5)
    deliver(0)

    def far_step(k, carry):
        produce(k)
        deliver(k)
        return carry

    def near_step(j, carry):
        produce(row_half + j)
        core_copy(row_half + j).start()
        with scope("fold"):
            fold_far(j)
        return carry

    def sum_step(j, carry):
        with scope("cross0"):
            cross_first(j)
        with scope("fold"):
            fold_near(row_half + j)

        @pl.when(row_half + j < last)
        def _():
            near_copy(row_half + j, 0).start()

        @pl.when(FIRST_SQUARES + j < LOADS)
        def _():
            with scope("squares"):
                square_batch(FIRST_SQUARES + j, 0)

        return carry

    lax.fori_loop(1, row_half, far_step, 0)
    lax.fori_loop(0, row_half, near_step, 0)
    high_go(2)
    lax.fori_loop(0, row_half, sum_step, 0)
    with scope("squares"):
        lax.fori_loop(min(FIRST_SQUARES + row_half, LOADS), LOADS, square_batch, 0)
    sq_first()
    for q in range(3, CHUNKS):
        high_go(q)

    def crosses(q):
        def near_go(k, carry):
            near_copy(k, q).start()
            return carry

        def cross_go(k, carry):
            cross(k, q)
            return carry

        with scope("crosses"):
            lax.fori_loop(row_half, last, near_go, 0)
            await_bytes(high_in.at[:, :, within(q)], high_recv.at[row_half + q - 1])
            lax.fori_loop(0, row_half, cross_go, 0)

    crosses(1)
    crosses(2)
    with scope("sq_second"):
        sq_second()
    for q in range(CHUNKS):
        row_in[q][s, every] = tiles[last, :, lines(q)]

    def owned(q, grp, n):
        j = grp * tile_dev + n
        total = row_in[q][source_of(0), places[0, j]]
        for k in range(1, row_count):
            total = total + row_in[q][source_of(k), places[k, j]]
        return total

    distant = ((1 - high) * 2 + (1 - low), (1 - high) * 2 + low)
    local = (partner, g)

    def b_copy(q, t):
        return send(part_b[q].at[t], in_b[q].at[t], b_send, b_recv.at[q * 2 + t], s, across)

    def c_copy(q):
        return send(part_c[q], in_c[q], c_send, c_recv.at[q], s, partner)

    arriving = 3 * row_count // 4 - 1

    def post(q):
        with scope("w_rows"):
            await_bytes(row_in[q].at[pl.ds(0, arriving), every], row_recv.at[q])
        with scope("post"):
            for t in range(2):
                def away(n, carry):
                    part_b[q][t, n] = owned(q, distant[t], n)
                    return carry

                lax.fori_loop(0, tile_dev, away, 0)
                b_copy(q, t).start()
            for t in range(2):
                def hold(n, carry):
                    held[q][t, n] = owned(q, local[t], n)
                    return carry

                lax.fori_loop(0, tile_dev, hold, 0)

    def store(place, values, scaled):
        out[:, place] = values * scale[:, place] if scaled else values

    def finish(q, scaled=False):
        with scope("w_b0"):
            b_copy(q, 0).wait_recv()
        part_c[q][...] = held[q][0] + in_b[q][0]
        c_copy(q).start()
        with scope("w_b1"):
            b_copy(q, 1).wait_recv()
        store(lines(q), held[q][1] + in_b[q][1], scaled)

    def collect(q, scaled=False):
        with scope("w_c"):
            c_copy(q).wait_recv()
        store(lines_from((1 - low) * tall + starts[q], sizes[q]), in_c[q][...], scaled)

    def factors():
        await_bytes(sq_total.at[pl.ds(0, 7 * nb8)], sq_recv.at[1])
        await_bytes(sq_parts.at[pl.ds(0, 7)], sq_send.at[1])
        sq_total[...] = jnp.sqrt(sq_total[...] / (rows_dev * row_count * grp_count) + epsilon)

        def factor(n, carry):
            pair = (s * region + g * tile_dev) + n
            left = sq_total[pair_blocks[0, pair]].reshape(1, width)
            right = sq_total[pair_blocks[1, pair]].reshape(1, width)
            left = jnp.broadcast_to(left, (width, width)).T
            scale[n] = 1.0 / (sample_count * left * right)
            return carry

        lax.fori_loop(0, tile_dev, factor, 0)

    def rescale(start, size):
        piece = lines_from(start, size)
        out[:, piece] = out[:, piece] * scale[:, piece]

    with scope("w_places"):
        place_copy.wait()
    post(0)
    crosses(3)
    post(1)
    finish(0)
    post(2)
    with scope("sq_third"):
        sq_third()
    finish(1)
    collect(0)
    post(3)
    finish(2)
    collect(1)
    with scope("factors"):
        factors()
    rescale(low * tall, starts[CHUNKS - 1])
    rescale((1 - low) * tall, starts[CHUNKS - 2])
    finish(CHUNKS - 1, True)
    collect(CHUNKS - 2, True)
    collect(CHUNKS - 1, True)

    with scope("drain"):
        await_bytes(core_in, core_send)
        await_bytes(first_in, first_send)
        await_bytes(high_in, high_send)
        await_bytes(tiles.at[pl.ds(0, arriving), every, pl.ds(0, tall)], row_send)
        await_bytes(tiles.at[pl.ds(0, tile_dev // cap), every, pl.ds(0, tall)], c_send)
        await_bytes(tiles.at[pl.ds(0, 2 * tile_dev // cap), every, pl.ds(0, tall)], b_send)
        await_bytes(sq_rows.at[pl.ds(0, row_half - 1)], near_send)
        await_bytes(sq_parts.at[pl.ds(0, 7)], sq_send.at[0])


def shards(matrix, sample_rows, pair_list, pair_count, pair_blocks):
    rows_dev, column_count = matrix.shape
    block_count, sample_count = sample_rows.shape[1:]
    width = column_count // block_count
    row_count = lax.axis_size("rows")
    grp_count = lax.axis_size("grp")
    cap = pair_list.shape[2]
    pairs = pair_blocks.shape[0]
    region = pairs // row_count
    tile_dev = region // grp_count
    half = cap // 2
    row_half = row_count // 2
    tall = width // 2
    sizes = [share * tall // sum(SHARES) for share in SHARES]
    nb8 = block_count // 8
    early = min(row_count, EARLY)
    dma = pltpu.SemaphoreType.DMA

    def vmem(*shape):
        return pltpu.VMEM(shape, F32)

    def smem(*shape):
        return pltpu.SMEM(shape, jnp.int32)

    dims = (row_count, grp_count, cap, pairs, block_count, width)
    return pl.pallas_call(
        functools.partial(kernel, dims),
        out_shape=pltpu.VMEM((tile_dev, width, width), F32),
        in_specs=[pl.BlockSpec(memory_space=pl.ANY) for _ in range(5)],
        out_specs=pl.BlockSpec(memory_space=pltpu.VMEM),
        scratch_shapes=[
            pltpu.VMEM((LOADS, rows_dev, column_count // LOADS), BF16),
            pltpu.VMEM((block_count, sample_count), jnp.int32),
            pltpu.VMEM((early, cap, rows_dev, width), BF16),
            smem(row_count, 128),
            vmem(row_count, cap, width, width),
            vmem(row_count, cap, tall, width),
            vmem(row_half, half, tall - sizes[0], width),
            vmem(row_half, 2, half, sizes[0], width),
            *[vmem(row_count, cap + 1, size, width) for size in sizes],
            *[vmem(2, tile_dev, size, width) for size in sizes],
            *[vmem(2, tile_dev, size, width) for size in sizes],
            *[vmem(2, tile_dev, size, width) for size in sizes],
            *[vmem(tile_dev, size, width) for size in sizes],
            *[vmem(tile_dev, size, width) for size in sizes],
            pltpu.VMEM((row_count, 128), jnp.int32),
            vmem(tile_dev, width, width),
            vmem(block_count, width), vmem(8, nb8, width), vmem(row_count, nb8, width),
            vmem(block_count, width),
            smem(row_count, cap, row_count), smem(row_count, row_count), smem(2, pairs),
            dma((3,)), dma, dma, dma((LOADS,)), dma((2,)), dma((2,)), dma, dma, dma, dma((row_count,)),
            dma, dma, dma((row_half + CHUNKS - 1,)), dma, dma((CHUNKS,)),
            dma, dma((2 * CHUNKS,)), dma, dma((CHUNKS,)),
        ],
        compiler_params=pltpu.CompilerParams(
            collective_id=0, has_side_effects=True, vmem_limit_bytes=60000000
        ),
        name="gram_tiles",
    )(pair_list.transpose(0, 2, 1), pair_count, pair_blocks.T, sample_rows[0], matrix)


def solution(mesh):
    in_specs = (P(("rows", "grp"), None), P(("rows", "grp"), None, None), P(), P(), P())
    out_specs = P(("rows", "grp"), None, None)
    return jax.shard_map(shards, mesh=mesh, in_specs=in_specs, out_specs=out_specs, check_vma=False)
```

time: 35.9 us -> 32.7 us (0.911)
  Pallas kernels: 34.9 us -> 31.7 us
    pallas_call x1, Pallas kernels: 34.9 us -> 31.7 us  [shards(): pl.pallas_call(functools.partial(kernel, dims), out_shape=pltpu.VMEM((til...]
where the time goes in v2:
time: 32.7 us; the launch traced here: 32.5 us
  Pallas kernels  31.7 us (97%)
  local copies, waits for them, and re-layouts  0.8 us (2%)
    pallas_call x1, Pallas kernels, shards(): pl.pallas_call(functools.partial(kernel, dims), out_shape=pltpu.VMEM((til...  31.7 us
    unnamed x1, local copies, waits for them, and re-layouts  0.8 us

profile of v2, /device:TPU:0, one launch (start us, length us, event | category | flops | bytes accessed | tf_op | source)
XLA Modules:
  0.0 32.5 jit_solution(7136084073096102410)
XLA Ops:
  0.0 31.7 %gram_tiles.1 = f32[8,128,128]{2,1,0:T(8,128)S(1)} custom-call(s32[8,4,8]{2,1,0:T(4,128)} %bitcast.4, s32[8,8]{1,0:T(8,128)} %count_hbm.1, s32[2,256]{1,0:T(2,128)} %bitcast.5, s32[128,256]{1,0:T(8,128)} %bitcast.3, bf16[320,16384]{1,0:T(8,128)(2,1)} %matrix.1), custom_call_target="tpu_custom_call" | custom-call | tf_op jit(solution)/shard_map/gram_tiles/pallas_call | solution.py:510
  31.7 0.8 %copy.7 = f32[8,128,128]{2,1,0:T(8,128)} copy(f32[8,128,128]{2,1,0:T(8,128)S(1)} %gram_tiles.1) | data formatting | bytes 1048576

commit v3 on v2

--- a/solution.py
+++ b/solution.py
@@ -348,8 +348,16 @@
 
     lax.fori_loop(1, row_half, far_step, 0)
     lax.fori_loop(0, row_half, near_step, 0)
-    high_go(2)
+    @pl.when(low == 0)
+    def _():
+        high_go(2)
+
     lax.fori_loop(0, row_half, sum_step, 0)
+
+    @pl.when(low == 1)
+    def _():
+        high_go(2)
+
     with scope("squares"):
         lax.fori_loop(min(FIRST_SQUARES + row_half, LOADS), LOADS, square_batch, 0)
     sq_first()
@@ -366,14 +374,19 @@
             return carry
 
         with scope("crosses"):
-            lax.fori_loop(row_half, last, near_go, 0)
+            @pl.when(low == 0)
+            def _():
+                lax.fori_loop(row_half, last, near_go, 0)
+
             await_bytes(high_in.at[:, :, within(q)], high_recv.at[row_half + q - 1])
             lax.fori_loop(0, row_half, cross_go, 0)
 
+            @pl.when(low == 1)
+            def _():
+                lax.fori_loop(row_half, last, near_go, 0)
+
     crosses(1)
     crosses(2)
-    with scope("sq_second"):
-        sq_second()
     for q in range(CHUNKS):
         row_in[q][s, every] = tiles[last, :, lines(q)]
 
@@ -452,7 +465,10 @@
     with scope("w_places"):
         place_copy.wait()
     post(0)
-    crosses(3)
+    with scope("sq_second"):
+        sq_second()
+    for q in range(3, CHUNKS):
+        crosses(q)
     post(1)
     finish(0)
     post(2)
@@ -460,9 +476,10 @@
         sq_third()
     finish(1)
     collect(0)
-    post(3)
-    finish(2)
-    collect(1)
+    for q in range(3, CHUNKS):
+        post(q)
+        finish(q - 1)
+        collect(q - 2)
     with scope("factors"):
         factors()
     rescale(low * tall, starts[CHUNKS - 1])

time: 32.7 us -> 32.3 us (0.988)
  no operation moved by 1% of the time
where the time goes in v3:
time: 32.3 us; the launch traced here: 32.2 us
  Pallas kernels  31.4 us (97%)
  local copies, waits for them, and re-layouts  0.8 us (2%)
    pallas_call x1, Pallas kernels, shards(): pl.pallas_call(functools.partial(kernel, dims), out_shape=pltpu.VMEM((til...  31.4 us
    unnamed x1, local copies, waits for them, and re-layouts  0.8 us

profile of v3, /device:TPU:0, one launch (start us, length us, event | category | flops | bytes accessed | tf_op | source)
XLA Modules:
  0.0 32.2 jit_solution(9008926877560023373)
XLA Ops:
  0.0 31.4 %gram_tiles.1 = f32[8,128,128]{2,1,0:T(8,128)S(1)} custom-call(s32[8,4,8]{2,1,0:T(4,128)} %bitcast.4, s32[8,8]{1,0:T(8,128)} %count_hbm.1, s32[2,256]{1,0:T(2,128)} %bitcast.5, s32[128,256]{1,0:T(8,128)} %bitcast.3, bf16[320,16384]{1,0:T(8,128)(2,1)} %matrix.1), custom_call_target="tpu_custom_call" | custom-call | tf_op jit(solution)/shard_map/gram_tiles/pallas_call | solution.py:527
  31.4 0.8 %copy.7 = f32[8,128,128]{2,1,0:T(8,128)} copy(f32[8,128,128]{2,1,0:T(8,128)S(1)} %gram_tiles.1) | data formatting | bytes 1048576

commit v4 on v3

--- a/solution.py
+++ b/solution.py
@@ -28,7 +28,7 @@
     row_in, part_b, in_b, held, part_c, in_c = [[next(it) for _ in range(CHUNKS)] for _ in range(6)]
     place_rows, scale, squares, sq_parts, sq_rows, sq_total = [next(it) for _ in range(6)]
     pair_list, pair_count, pair_blocks = [next(it) for _ in range(3)]
-    (table_sem, sample_sem, place_sem, load_sem, sq_send, sq_recv, near_send, near_recv, core_send, core_recv,
+    (table_sem, sample_sem, load_sem, sq_send, sq_recv, near_send, near_recv, core_send, core_recv,
      first_send, high_send, high_recv, row_send, row_recv, b_send, b_recv, c_send, c_recv) = it
 
     batch = block_count // LOADS
@@ -94,14 +94,14 @@
             table.start()
         wide = batch * width
         for i in range(LOADS):
-            pltpu.make_async_copy(matrix.at[:, pl.ds(i * wide, wide)], mat.at[i], load_sem.at[i]).start(priority=1)
+            pltpu.make_async_copy(matrix.at[:, pl.ds(i * wide, wide)], mat.at[i], load_sem.at[min(i, FIRST_SQUARES)]).start(priority=1)
 
     def owner_of(k):
         other = 1 - lax.div(k, row_half)
         j = k + 1 - other
         return (top * (1 - other) + (1 - top) * other) * row_half + lax.rem(s + j, row_half)
 
-    place_copy = pltpu.make_async_copy(place_rows, places, place_sem)
+    place_copy = pltpu.make_async_copy(place_rows, places, sample_sem)
 
     def fill_places():
         pair = s * region + lax.broadcasted_iota(jnp.int32, (1, place_rows.shape[1]), 1)
@@ -167,14 +167,10 @@
             await_bytes(mat.at[i], load_sem.at[i])
         return square_batch(i, carry)
 
-    def load_wait(i, carry):
-        await_bytes(mat.at[i], load_sem.at[i])
-        return carry
-
     with scope("load_sq"):
         lax.fori_loop(0, FIRST_SQUARES, load_batch, 0)
     with scope("load_rest"):
-        lax.fori_loop(FIRST_SQUARES, LOADS, load_wait, 0)
+        await_bytes(mat.at[pl.ds(FIRST_SQUARES, LOADS - FIRST_SQUARES)], load_sem.at[FIRST_SQUARES])
 
     nb8 = block_count // 8
     side = lax.rem(s, 2)
@@ -401,7 +397,7 @@
     local = (partner, g)
 
     def b_copy(q, t):
-        return send(part_b[q].at[t], in_b[q].at[t], b_send, b_recv.at[q * 2 + t], s, across)
+        return send(part_b[q].at[t], in_b[q].at[t], b_send, b_recv.at[q if q < CHUNKS - 1 else q + t], s, across)
 
     def c_copy(q):
         return send(part_c[q], in_c[q], c_send, c_recv.at[q], s, partner)
@@ -431,11 +427,15 @@
 
     def finish(q, scaled=False):
         with scope("w_b0"):
-            b_copy(q, 0).wait_recv()
+            if q < CHUNKS - 1:
+                await_bytes(in_b[q], b_recv.at[q])
+            else:
+                b_copy(q, 0).wait_recv()
         part_c[q][...] = held[q][0] + in_b[q][0]
         c_copy(q).start()
-        with scope("w_b1"):
-            b_copy(q, 1).wait_recv()
+        if q == CHUNKS - 1:
+            with scope("w_b1"):
+                b_copy(q, 1).wait_recv()
         store(lines(q), held[q][1] + in_b[q][1], scaled)
 
     def collect(q, scaled=False):
@@ -549,9 +549,9 @@
             vmem(block_count, width), vmem(8, nb8, width), vmem(row_count, nb8, width),
             vmem(block_count, width),
             smem(row_count, cap, row_count), smem(row_count, row_count), smem(2, pairs),
-            dma((3,)), dma, dma, dma((LOADS,)), dma((2,)), dma((2,)), dma, dma, dma, dma((row_count,)),
+            dma((3,)), dma, dma((FIRST_SQUARES + 1,)), dma((2,)), dma((2,)), dma, dma, dma, dma((row_count,)),
             dma, dma, dma((row_half + CHUNKS - 1,)), dma, dma((CHUNKS,)),
-            dma, dma((2 * CHUNKS,)), dma, dma((CHUNKS,)),
+            dma, dma((CHUNKS + 1,)), dma, dma((CHUNKS,)),
         ],
         compiler_params=pltpu.CompilerParams(
             collective_id=0, has_side_effects=True, vmem_limit_bytes=60000000

time: 32.3 us -> 32.2 us (level)
  no operation moved by 1% of the time
where the time goes in v4:
time: 32.2 us; the launch traced here: 32.1 us
  Pallas kernels  31.3 us (97%)
  local copies, waits for them, and re-layouts  0.8 us (2%)
    pallas_call x1, Pallas kernels, shards(): pl.pallas_call(functools.partial(kernel, dims), out_shape=pltpu.VMEM((til...  31.3 us
    unnamed x1, local copies, waits for them, and re-layouts  0.8 us

profile of v4, /device:TPU:0, one launch (start us, length us, event | category | flops | bytes accessed | tf_op | source)
XLA Modules:
  0.0 32.1 jit_solution(208783962713935407)
XLA Ops:
  0.0 31.3 %gram_tiles.1 = f32[8,128,128]{2,1,0:T(8,128)S(1)} custom-call(s32[8,4,8]{2,1,0:T(4,128)} %bitcast.4, s32[8,8]{1,0:T(8,128)} %count_hbm.1, s32[2,256]{1,0:T(2,128)} %bitcast.5, s32[128,256]{1,0:T(8,128)} %bitcast.3, bf16[320,16384]{1,0:T(8,128)(2,1)} %matrix.1), custom_call_target="tpu_custom_call" | custom-call | tf_op jit(solution)/shard_map/gram_tiles/pallas_call | solution.py:527
  31.3 0.8 %copy.7 = f32[8,128,128]{2,1,0:T(8,128)} copy(f32[8,128,128]{2,1,0:T(8,128)S(1)} %gram_tiles.1) | data formatting | bytes 1048576

commit v5 on v4

--- a/solution.py
+++ b/solution.py
@@ -396,8 +396,8 @@
     distant = ((1 - high) * 2 + (1 - low), (1 - high) * 2 + low)
     local = (partner, g)
 
-    def b_copy(q, t):
-        return send(part_b[q].at[t], in_b[q].at[t], b_send, b_recv.at[q if q < CHUNKS - 1 else q + t], s, across)
+    def b_copy(q, t, which):
+        return send(part_b[q].at[t, which], in_b[q].at[t, which], b_send, b_recv.at[q if q < CHUNKS - 1 else q + t], s, across)
 
     def c_copy(q):
         return send(part_c[q], in_c[q], c_send, c_recv.at[q], s, partner)
@@ -413,8 +413,11 @@
                     part_b[q][t, n] = owned(q, distant[t], n)
                     return carry
 
-                lax.fori_loop(0, tile_dev, away, 0)
-                b_copy(q, t).start()
+                pieces = 2 if q == CHUNKS - 1 else 1
+                for c in range(pieces):
+                    size = tile_dev // pieces
+                    lax.fori_loop(c * size, (c + 1) * size, away, 0)
+                    b_copy(q, t, pl.ds(c * size, size)).start()
             for t in range(2):
                 def hold(n, carry):
                     held[q][t, n] = owned(q, local[t], n)
@@ -430,12 +433,12 @@
             if q < CHUNKS - 1:
                 await_bytes(in_b[q], b_recv.at[q])
             else:
-                b_copy(q, 0).wait_recv()
+                await_bytes(in_b[q].at[0], b_recv.at[q])
         part_c[q][...] = held[q][0] + in_b[q][0]
         c_copy(q).start()
         if q == CHUNKS - 1:
             with scope("w_b1"):
-                b_copy(q, 1).wait_recv()
+                await_bytes(in_b[q].at[1], b_recv.at[q + 1])
         store(lines(q), held[q][1] + in_b[q][1], scaled)
 
     def collect(q, scaled=False):

time: 32.2 us -> 32.2 us (level)
  no operation moved by 1% of the time
where the time goes in v5:
time: 32.2 us; the launch traced here: 32.1 us
  Pallas kernels  31.3 us (97%)
  local copies, waits for them, and re-layouts  0.8 us (2%)
    pallas_call x1, Pallas kernels, shards(): pl.pallas_call(functools.partial(kernel, dims), out_shape=pltpu.VMEM((til...  31.3 us
    unnamed x1, local copies, waits for them, and re-layouts  0.8 us

profile of v5, /device:TPU:0, one launch (start us, length us, event | category | flops | bytes accessed | tf_op | source)
XLA Modules:
  0.0 32.1 jit_solution(18199360111380079062)
XLA Ops:
  0.0 31.3 %gram_tiles.1 = f32[8,128,128]{2,1,0:T(8,128)S(1)} custom-call(s32[8,4,8]{2,1,0:T(4,128)} %bitcast.4, s32[8,8]{1,0:T(8,128)} %count_hbm.1, s32[2,256]{1,0:T(2,128)} %bitcast.5, s32[128,256]{1,0:T(8,128)} %bitcast.3, bf16[320,16384]{1,0:T(8,128)(2,1)} %matrix.1), custom_call_target="tpu_custom_call" | custom-call | tf_op jit(solution)/shard_map/gram_tiles/pallas_call | solution.py:530
  31.3 0.8 %copy.7 = f32[8,128,128]{2,1,0:T(8,128)} copy(f32[8,128,128]{2,1,0:T(8,128)S(1)} %gram_tiles.1) | data formatting | bytes 1048576
